TPU v7x, 8 devices: a whole 2x2x1 slice. The times are simulated.
8 devices in a mesh: dp: 2 (over z, y), tp: 4 (over x, core).
Axes of the slice: x: 2, y: 2, z: 1, core: 2. Of those that a mesh axis runs over, the one named last changes fastest.
Arguments:
- hidden: bfloat16 [8, 1024, 2560], P('dp', 'tp'), parts along dimension 0
- ln1_gain: float32 [2560], replicated
- ln1_bias: float32 [2560], replicated
- w_qkv: bfloat16 [2560, 3, 32, 80], P(None, None, 'tp')
- b_qkv: bfloat16 [3, 32, 80], P(None, 'tp')
- w_out: bfloat16 [32, 80, 2560], P('tp')
- b_out: bfloat16 [2560], replicated
- ln2_gain: float32 [2560], replicated
- ln2_bias: float32 [2560], replicated
- w_up: bfloat16 [2560, 10240], P(None, 'tp')
- b_up: bfloat16 [10240], P('tp')
- w_down: bfloat16 [10240, 2560], P('tp')
- b_down: bfloat16 [2560], replicated
Outputs:
- output: bfloat16 [8, 1024, 2560], P('dp', 'tp'), parts along dimension 0
There are 2 independent parts. A program takes and returns all parts, laid end to end along the dimension named above; an argument that names none is the same for every part.
All inputs are finite; a program needn't handle non-finite values.
Results may differ from a plain program's by a relative error of at most 0.0106374.
Values are sent between devices in bfloat16 or wider.
A program may use at most 1 GiB of HBM per device.

v0:
```python
import jax
import jax.numpy as jnp
from jax import lax
from jax.sharding import PartitionSpec as P

LN_EPS = 1e-5


def layer_norm(inputs, gain_vec, shift_vec):
    as_f32 = inputs.astype(jnp.float32)
    row_mean = jnp.mean(as_f32, axis=-1, keepdims=True)
    centered = as_f32 - row_mean
    variance = jnp.mean(centered * centered, axis=-1, keepdims=True)
    return (centered * lax.rsqrt(variance + LN_EPS) * gain_vec + shift_vec).astype(jnp.bfloat16)


def causal_attention(queries, keys_all, values):
    seq_len = queries.shape[1]
    head_dim = queries.shape[3]
    logits = jnp.einsum("bqhd,bkhd->bhqk", queries, keys_all, preferred_element_type=jnp.float32) * head_dim ** -0.5
    causal = lax.broadcasted_iota(jnp.int32, (seq_len, seq_len), 0) >= lax.broadcasted_iota(jnp.int32, (seq_len, seq_len), 1)
    logits = jnp.where(causal, logits, -1e30)
    row_max = jnp.max(logits, axis=-1, keepdims=True)
    exp_vals = jnp.exp(logits - row_max)
    weights_bf = (exp_vals / jnp.sum(exp_vals, axis=-1, keepdims=True)).astype(jnp.bfloat16)
    return jnp.einsum("bhqk,bkhd->bqhd", weights_bf, values, preferred_element_type=jnp.float32).astype(jnp.bfloat16)


def solution(mesh):
    group_size = mesh.shape["tp"]

    def scatter_sum(partial):
        n_batch, seq_len, feat_dim = partial.shape
        split_view = partial.astype(jnp.bfloat16).reshape(n_batch, group_size, seq_len // group_size, feat_dim)
        received = lax.all_to_all(split_view, "tp", 1, 1, tiled=True)
        return jnp.sum(received.astype(jnp.float32), axis=1)

    def device_body(hidden, ln1_gain, ln1_bias, w_qkv, b_qkv, w_out, b_out, ln2_gain, ln2_bias, w_up, b_up, w_down, b_down):
        normed = layer_norm(hidden, ln1_gain, ln1_bias)
        normed_all = lax.all_gather(normed, "tp", axis=1, tiled=True)
        qkv_acc = jnp.einsum("bsd,dthe->bsthe", normed_all, w_qkv, preferred_element_type=jnp.float32)
        qkv_all = (qkv_acc + b_qkv.astype(jnp.float32)).astype(jnp.bfloat16)
        context = causal_attention(qkv_all[:, :, 0], qkv_all[:, :, 1], qkv_all[:, :, 2])
        attn_part = jnp.einsum("bqhd,hde->bqe", context, w_out, preferred_element_type=jnp.float32)
        attn_sum = scatter_sum(attn_part)
        resid_mid = (hidden.astype(jnp.float32) + (attn_sum + b_out.astype(jnp.float32))).astype(jnp.bfloat16)
        normed_mid = layer_norm(resid_mid, ln2_gain, ln2_bias)
        mid_all = lax.all_gather(normed_mid, "tp", axis=1, tiled=True)
        up_proj = jnp.einsum("bsd,df->bsf", mid_all, w_up, preferred_element_type=jnp.float32) + b_up.astype(jnp.float32)
        gelu_out = jax.nn.gelu(up_proj, approximate=True).astype(jnp.bfloat16)
        down_part = jnp.einsum("bsf,fd->bsd", gelu_out, w_down, preferred_element_type=jnp.float32)
        down_sum = scatter_sum(down_part)
        return (resid_mid.astype(jnp.float32) + (down_sum + b_down.astype(jnp.float32))).astype(jnp.bfloat16)

    in_layout = (P("dp", "tp", None), P(), P(), P(None, None, "tp", None), P(None, "tp", None), P("tp", None, None), P(), P(), P(), P(None, "tp"), P("tp"), P("tp", None), P())
    layer_fn = jax.shard_map(device_body, mesh=mesh, in_specs=in_layout, out_specs=P("dp", "tp", None), check_vma=False)
    return layer_fn
```

profile of v0, /device:TPU:0, one launch (start us, length us, event | category | flops | bytes accessed | tf_op | source)
XLA Modules:
  0.0 1161.7 jit_solution(14813332189693762777)
XLA Ops:
  6.5 0.0 copy-start
  6.5 0.0 copy-start.5
  6.5 0.0 all-gather.3.cloned.1.call-start
  6.5 0.0 copy-start.2
  6.5 3.4 convert_reduce_fusion.3
  10.0 4.1 fusion.28
  14.1 0.0 copy-done.2
  14.1 5.1 fusion.31
  19.2 0.0 all-gather.3.cloned.1.call-update
  19.2 0.0 copy-done.5
  19.2 1.3 iota_compare_fusion
  20.5 130.1 %all-gather.3.cloned.1.call-done = bf16[4,1024,2560]{2,1,0:T(8,128)(2,1)} async-done(((bf16[4,256,2560]{2,1,0:T(8,128)(2,1)}), bf16[4,1024,2560]{2,1,0:T(8,128)(2,1)}) %all-gather.3.cloned.1.call-update) | async-done | bytes 20971536 | tf_op jit(solution)/shard_map/all_gather | solution.py:40
  150.7 49.1 %add_convert_fusion = bf16[4,1024,3,8,80]{1,4,3,2,0:T(8,128)(2,1)} fusion(f32[3,8,80]{2,1,0:T(8,128)S(1)} %convert_element_type.61, bf16[4,1024,2560]{2,1,0:T(8,128)(2,1)} %all-gather.3.cloned.1.call-done, bf16[2560,3,8,80]{0,3,2,1:T(8,128)(2,1)} %param.16), kind=kOutput, calls=%fused_computation.21 | convolution fusion | flops 40281047040 | bytes 46538240 | tf_op jit(solution)/shard_map/bsd,dthe->bsthe/dot_general | solution.py:41
  199.7 60.3 %fusion.44 = (f32[4,8,1024]{2,1,0:T(8,128)S(1)}, f32[4,8,1024,1024]{2,3,1,0:T(8,128)}) fusion(pred[1024,1024]{0,1:T(8,128)(4,1)} %iota_compare_fusion, bf16[4,1024,3,8,80]{1,4,3,2,0:T(8,128)(2,1)} %add_convert_fusion), kind=kOutput, calls=%fused_computation.63 | convolution fusion | flops 5502927872 | bytes 145883136 | tf_op jit(solution)/shard_map/sub | solution.py:24
  260.0 0.0 copy-done
  260.0 64.7 %bitcast_convert_fusion = bf16[4,1024,2560]{2,1,0:T(8,128)(2,1)} fusion(bf16[8,80,2560]{2,1,0:T(8,128)(2,1)S(1)} %copy-done, f32[4,8,1024,1024]{2,3,1,0:T(8,128)} %get-tuple-element.8, f32[4,8,1024]{2,1,0:T(8,128)S(1)} %get-tuple-element.7, bf16[4,1024,3,8,80]{1,4,3,2,0:T(8,128)(2,1)} %add_convert_fusion), kind=kOutput, calls=%fused_computation.18 | convolution fusion | flops 18870697984 | bytes 163840000 | tf_op jit(solution)/shard_map/bqhd,hde->bqe/dot_general | solution.py:44
  324.7 17.5 %copy.14 = bf16[4,4,256,2560]{3,2,0,1:T(8,128)(2,1)} copy(bf16[4,4,256,2560]{3,2,1,0:T(8,128)(2,1)} %bitcast.64) | data formatting | bytes 41943040 | tf_op jit(solution)/shard_map/reshape | solution.py:34
  342.2 0.0 copy-start.6
  342.2 7.8 all-to-all-start
  350.1 0.0 all-gather.5.cloned.1.call-start
  350.1 0.0 copy-done.6
  350.1 227.9 %all-to-all-done = bf16[4,4,256,2560]{3,2,0,1:T(8,128)(2,1)} async-done(((bf16[4,4,256,2560]{3,2,0,1:T(8,128)(2,1)}), bf16[4,4,256,2560]{3,2,0,1:T(8,128)(2,1)}, u32[]{:S(2)}, u32[]{:S(2)}) %all-to-all-start) | async-done | bytes 20971552 | tf_op jit(solution)/shard_map/all_to_all | solution.py:35
  578.0 15.9 %convert_reduce_fusion.1 = f32[4,256,2560]{2,1,0:T(8,128)} fusion(bf16[4,4,256,2560]{3,2,0,1:T(8,128)(2,1)} %all-to-all-done), kind=kLoop, calls=%fused_computation.20 | loop fusion | flops 18350080 | bytes 31457280 | tf_op jit(solution)/shard_map/reduce_sum | solution.py:36
  593.9 0.0 copy-start.3
  594.0 0.0 copy-start.4
  594.0 9.8 convert_reduce_fusion.2
  603.7 0.0 copy-start.7
  603.7 4.0 fusion.24
  607.7 0.0 copy-done.3
  607.7 0.0 copy-done.4
  607.8 6.8 fusion.27
  614.5 0.0 all-gather.5.cloned.1.call-update
  614.6 0.0 copy-done.7
  614.6 128.6 %all-gather.5.cloned.1.call-done = bf16[4,1024,2560]{2,1,0:T(8,128)(2,1)} async-done(((bf16[4,256,2560]{2,1,0:T(8,128)(2,1)}), bf16[4,1024,2560]{2,1,0:T(8,128)(2,1)}) %all-gather.5.cloned.1.call-update) | async-done | bytes 20971536 | tf_op jit(solution)/shard_map/all_gather | solution.py:48
  743.2 69.9 %fusion.13 = bf16[4,1024,2560]{2,1,0:T(8,128)(2,1)} fusion(bf16[4,1024,2560]{2,1,0:T(8,128)(2,1)} %all-gather.5.cloned.1.call-done, f32[2560]{0:T(1024)S(1)} %convert_element_type.72, bf16[2560,2560]{1,0:T(8,128)(2,1)} %param.22), kind=kOutput, calls=%fused_computation.17 | convolution fusion | flops 53791948800 | bytes 55060480 | tf_op jit(solution)/shard_map/bsd,df->bsf/dot_general | solution.py:49
  813.1 62.5 %convolution_convert_fusion = bf16[4,1024,2560]{2,1,0:T(8,128)(2,1)} fusion(bf16[4,1024,2560]{2,1,0:T(8,128)(2,1)} %fusion.13, bf16[2560,2560]{1,0:T(8,128)(2,1)} %param.24), kind=kOutput, calls=%fused_computation.24 | convolution fusion | flops 53697576960 | bytes 55050240 | tf_op jit(solution)/shard_map/bsf,fd->bsd/dot_general | solution.py:51
  875.6 17.5 %copy.15 = bf16[4,4,256,2560]{3,2,0,1:T(8,128)(2,1)} copy(bf16[4,4,256,2560]{3,2,1,0:T(8,128)(2,1)} %bitcast.65) | data formatting | bytes 41943040 | tf_op jit(solution)/shard_map/reshape | solution.py:34
  893.1 0.0 copy-start.8
  893.1 7.8 all-to-all-start.1
  900.9 0.0 copy-done.8
  900.9 227.9 %all-to-all-done.1 = bf16[4,4,256,2560]{3,2,0,1:T(8,128)(2,1)} async-done(((bf16[4,4,256,2560]{3,2,0,1:T(8,128)(2,1)}), bf16[4,4,256,2560]{3,2,0,1:T(8,128)(2,1)}, u32[]{:S(2)}, u32[]{:S(2)}) %all-to-all-start.1) | async-done | bytes 20971552 | tf_op jit(solution)/shard_map/all_to_all | solution.py:35
  1128.9 0.0 copy-start.1
  1128.9 16.1 %convert_reduce_fusion = f32[4,256,2560]{2,1,0:T(8,128)} fusion(bf16[4,4,256,2560]{3,2,0,1:T(8,128)(2,1)} %all-to-all-done.1), kind=kLoop, calls=%fused_computation.19 | loop fusion | flops 18350080 | bytes 31457280 | tf_op jit(solution)/shard_map/reduce_sum | solution.py:36
  1145.0 9.6 fusion.33
  1154.6 0.0 copy-done.1
  (8 shorter events, 0.0 us)
Async XLA Ops:
  6.5 253.5 %copy-start = (bf16[8,80,2560]{2,1,0:T(8,128)(2,1)S(1)}, bf16[8,80,2560]{2,1,0:T(8,128)(2,1)}, u32[]{:S(2)}) copy-start(bf16[8,80,2560]{2,1,0:T(8,128)(2,1)} %param.18) | copy-start | bytes 9830404
  6.5 12.7 %copy-start.5 = (bf16[3,8,80]{2,1,0:T(8,128)(2,1)S(1)}, bf16[3,8,80]{2,1,0:T(8,128)(2,1)}, u32[]{:S(2)}) copy-start(bf16[3,8,80]{2,1,0:T(8,128)(2,1)} %param.17) | copy-start | bytes 11524
  6.5 144.1 %all-gather.3.cloned.1.call-start = ((), (), s32[]{:S(2)}) async-start(), calls=%async_computation.2 | async-start | bytes 26214400 | tf_op jit(solution)/shard_map/all_gather | solution.py:40
  6.5 7.6 copy-start.2
  342.2 7.9 copy-start.6
  342.2 235.8 %all-to-all-start = ((bf16[4,4,256,2560]{3,2,0,1:T(8,128)(2,1)}), bf16[4,4,256,2560]{3,2,0,1:T(8,128)(2,1)}, u32[]{:S(2)}, u32[]{:S(2)}) async-start(bf16[4,4,256,2560]{3,2,0,1:T(8,128)(2,1)} %copy.14), calls=%async_computation | async-start | bytes 41943040 | tf_op jit(solution)/shard_map/all_to_all | solution.py:35
  350.1 393.2 %all-gather.5.cloned.1.call-start = ((), (), s32[]{:S(2)}) async-start(), calls=%async_computation.3 | async-start | bytes 26214400 | tf_op jit(solution)/shard_map/all_gather | solution.py:48
  593.9 13.8 %copy-start.3 = (f32[2560]{0:T(1024)S(1)}, f32[2560]{0:T(1024)}, u32[]{:S(2)}) copy-start(f32[2560]{0:T(1024)} %param.21) | copy-start | bytes 30724
  594.0 13.8 %copy-start.4 = (f32[2560]{0:T(1024)S(1)}, f32[2560]{0:T(1024)}, u32[]{:S(2)}) copy-start(f32[2560]{0:T(1024)} %param.20) | copy-start | bytes 30724
  603.7 10.8 copy-start.7
  893.1 7.9 copy-start.8
  893.1 235.8 %all-to-all-start.1 = ((bf16[4,4,256,2560]{3,2,0,1:T(8,128)(2,1)}), bf16[4,4,256,2560]{3,2,0,1:T(8,128)(2,1)}, u32[]{:S(2)}, u32[]{:S(2)}) async-start(bf16[4,4,256,2560]{3,2,0,1:T(8,128)(2,1)} %copy.15), calls=%async_computation.1 | async-start | bytes 41943040 | tf_op jit(solution)/shard_map/all_to_all | solution.py:35
  1128.9 25.8 %copy-start.1 = (bf16[8,80,2560]{2,1,0:T(8,128)(2,1)S(1)}, bf16[8,80,2560]{2,1,0:T(8,128)(2,1)}, u32[]{:S(2)}) copy-start(bf16[8,80,2560]{2,1,0:T(8,128)(2,1)} %param.18) | copy-start | bytes 9830404
Sparse Core Ops, SparseCore 0:
  19.3 131.2 all-gather.2
  614.7 128.4 all-gather.4
where the time goes:
time: 1170 us; the launch traced here: 1160 us
  waiting for transfers between devices  715 us (61%)
  matrix products  306 us (26%)
  other arithmetic  76.2 us (7%)
  local copies, waits for them, and re-layouts  35 us (3%)
  starting transfers between devices  15.7 us (1%)
  between operations  13.8 us (1%)
    all_to_all x2, waiting for transfers between devices, scatter_sum(): received = lax.all_to_all(split_view, 'tp', 1, 1, tiled=True)  456 us
    all_gather x1, waiting for transfers between devices, device_body(): normed_all = lax.all_gather(normed, 'tp', axis=1, tiled=True)  130 us
    all_gather x1, waiting for transfers between devices, device_body(): mid_all = lax.all_gather(normed_mid, 'tp', axis=1, tiled=True)  129 us
    dot_general x1, matrix products, device_body(): jnp.einsum('bsd,df->bsf', mid_all, w_up, preferred_element_type=jnp.float32)  69.9 us
    dot_general x1, matrix products, device_body(): jnp.einsum('bqhd,hde->bqe', context, w_out, preferred_element_type=jnp.fl...  64.7 us
    dot_general x1, matrix products, device_body(): jnp.einsum('bsf,fd->bsd', gelu_out, w_down, preferred_element_type=jnp.fl...  62.5 us
    sub x1, matrix products, causal_attention(): exp_vals = jnp.exp(logits - row_max)  60.3 us
    dot_general x1, matrix products, device_body(): jnp.einsum('bsd,dthe->bsthe', normed_all, w_qkv, preferred_element_type=j...  49.1 us
  transfers between devices with their start and end apart: 4, of which 4 were waited for; matrix products, arithmetic and copies ran while one was open for 0% of the time, Pallas kernels for 0%

commit v1 on v0

v1 whole, which is shorter than its diff:
```python
import functools
import math

import jax
import jax.numpy as jnp
from jax import lax
from jax.experimental import pallas as pl
from jax.experimental.pallas import tpu as pltpu
from jax.sharding import PartitionSpec as P


LN_EPS = 1e-5
BF16 = jnp.bfloat16
F32 = jnp.float32


CHUNK = 64
VMEM_MIB = 60
ANY = pl.BlockSpec(memory_space=pl.ANY)
WHOLE = pl.BlockSpec(memory_space=pltpu.VMEM)
SMEM = pl.BlockSpec(memory_space=pltpu.SMEM)


def normalize(x, gain, shift):
    as_f32 = x.astype(F32)
    row_mean = jnp.mean(as_f32, axis=-1, keepdims=True)
    centered = as_f32 - row_mean
    variance = jnp.mean(centered * centered, axis=-1, keepdims=True)
    return (centered * lax.rsqrt(variance + LN_EPS) * gain + shift).astype(BF16)


def params(**kwargs):
    return pltpu.CompilerParams(vmem_limit_bytes=VMEM_MIB << 20, **kwargs)


def cost(flops, moved, transcendentals=0):
    return pl.CostEstimate(flops=flops, bytes_accessed=moved, transcendentals=transcendentals)


def qkv_kernel(n_x, n_w, tile, *refs):
    x_refs, refs = refs[:n_x], refs[n_x:]
    gain_ref, shift_ref, bias_ref, refs = refs[0], refs[1], refs[2], refs[3:]
    w_refs, (out_ref, x_buf, normed, w_buf, x_sem, w_sem) = refs[:n_w], refs[n_w:]
    block = x_refs[0].shape[1]
    sub = tile // 2
    per_w = w_refs[0].shape[0] // sub
    steps = n_w * per_w // 2

    def fetch(n, go):
        slot = lax.rem(n, 2)
        for h in range(2):
            q = 2 * n + h
            if not go:
                pltpu.make_async_copy(w_refs[0].at[pl.ds(0, sub)], w_buf.at[slot, pl.ds(h * sub, sub)], w_sem.at[slot, h]).wait()
                continue
            for t in range(n_w):
                @pl.when((q >= t * per_w) & (q < (t + 1) * per_w))
                def _():
                    rows = pl.ds(pl.multiple_of((q - t * per_w) * sub, sub), sub)
                    pltpu.make_async_copy(w_refs[t].at[rows], w_buf.at[slot, pl.ds(h * sub, sub)], w_sem.at[slot, h]).start()

    copies = [pltpu.make_async_copy(x_refs[p].at[0], x_buf.at[pl.ds(p * block, block)], x_sem.at[p]) for p in range(n_x)]
    for c in copies:
        c.start()
    fetch(0, True)
    for p, c in enumerate(copies):
        c.wait()

        @pl.loop(0, block // CHUNK)
        def _(r):
            rows = pl.ds(pl.multiple_of(p * block + r * CHUNK, CHUNK), CHUNK)
            normed[rows, :] = normalize(x_buf[rows, :], gain_ref[...], shift_ref[...])

    @pl.loop(0, steps)
    def _(n):
        @pl.when(n + 1 < steps)
        def _():
            fetch(n + 1, True)

        fetch(n, False)
        acc = lax.dot_general(normed[...], w_buf[lax.rem(n, 2)], (((1,), (1,)), ((), ())), preferred_element_type=F32)
        cols = pl.ds(pl.multiple_of(n * tile, tile), tile)
        out = (acc + bias_ref[:, cols].astype(F32)).astype(BF16)
        out_ref[:, :, cols] = out.reshape(n_x, block, tile)


def qkv_projection(xs, gain, shift, bias, ws):
    n_x, n_w = len(xs), len(ws)
    _, block, d_model = xs[0].shape
    n_cols = n_w * ws[0].shape[0]
    tile = 768
    return pl.pallas_call(
        functools.partial(qkv_kernel, n_x, n_w, tile),
        out_shape=jax.ShapeDtypeStruct((n_x, block, n_cols), BF16),
        in_specs=[ANY] * n_x + [WHOLE] * 3 + [ANY] * n_w,
        out_specs=WHOLE,
        scratch_shapes=[
            pltpu.VMEM((n_x * block, d_model), BF16),
            pltpu.VMEM((n_x * block, d_model), BF16),
            pltpu.VMEM((2, tile, d_model), BF16),
            pltpu.SemaphoreType.DMA((n_x,)),
            pltpu.SemaphoreType.DMA((2, 2)),
        ],
        compiler_params=params(),
        cost_estimate=cost(2 * n_x * block * d_model * n_cols, 2 * (n_x * block * (d_model + n_cols) + n_cols * d_model)),
    )(*xs, gain, shift, bias, *ws)


def attention_kernel(n_heads, head_dim, window, me_ref, local_ref, remote_ref, near_ref, far_ref, ordered, ctx_ref):
    head = pl.program_id(1)
    me = me_ref[0]
    n_slots, block, width = ctx_ref.shape
    half = n_slots // 2

    @pl.when(head == 0)
    def _():
        for slot in range(n_slots):
            source = local_ref if slot < half else remote_ref
            ordered[me ^ slot] = source[slot % half]

    first = head * head_dim
    start = jnp.minimum((first // 128) * 128, width - window)
    start = pl.multiple_of(start, 128)
    lane = lax.broadcasted_iota(jnp.int32, (block, window), 1) + start
    in_head = (lane >= first) & (lane < first + head_dim)
    to_exp2 = head_dim ** -0.5 * math.log2(math.e)
    rows = lax.broadcasted_iota(jnp.int32, (block, block), 0)
    cols = lax.broadcasted_iota(jnp.int32, (block, block), 1)
    contract_last = (((1,), (1,)), ((), ()))
    for g in range(n_slots):
        q = ordered[g, :, pl.ds(start, window)]
        q = jnp.where(in_head, q, jnp.zeros_like(q))
        diag_k = ordered[g, :, pl.ds(width + start, window)]
        diag = lax.dot_general(q, diag_k, contract_last, preferred_element_type=F32)
        diag = jnp.where(rows >= cols, diag, -1e30)
        row_max = jnp.max(diag, axis=-1, keepdims=True)
        if g:
            k = ordered[0:g, :, pl.ds(width + start, window)].reshape(g * block, window)
            full = lax.dot_general(q, k, contract_last, preferred_element_type=F32)
            row_max = jnp.maximum(row_max, jnp.max(full, axis=-1, keepdims=True))
        diag = jnp.exp2((diag - row_max) * to_exp2)
        total = jnp.sum(diag, axis=-1, keepdims=True)
        if g:
            full = jnp.exp2((full - row_max) * to_exp2)
            total = total + jnp.sum(full, axis=-1, keepdims=True)
        inverse = 1.0 / total
        diag_v = ordered[g, :, pl.ds(2 * width + start, window)]
        ctx = jnp.dot((diag * inverse).astype(BF16), diag_v, preferred_element_type=F32)
        if g:
            v = ordered[0:g, :, pl.ds(2 * width + start, window)].reshape(g * block, window)
            ctx = ctx + jnp.dot((full * inverse).astype(BF16), v, preferred_element_type=F32)
        slot = me ^ g
        old = ctx_ref[slot, :, pl.ds(start, window)]
        ctx_ref[slot, :, pl.ds(start, window)] = jnp.where(in_head, ctx.astype(BF16), old)

    @pl.when(head == n_heads - 1)
    def _():
        near_ref[...] = ctx_ref[0:half]
        far_ref[...] = ctx_ref[half:]


def attention(me, qkv_local, local_at, qkv_remote, n_groups, n_heads, head_dim):
    n_half, block, columns = qkv_remote.shape
    three_width = columns // n_groups
    width = three_width // 3
    n_slots = 2 * n_half
    window = 256
    pairs = n_groups * n_heads * n_slots * (n_slots + 1) // 2
    out = jax.ShapeDtypeStruct((n_half, block, n_groups * width), BF16)
    return pl.pallas_call(
        functools.partial(attention_kernel, n_heads, head_dim, window),
        out_shape=[out, out],
        grid_spec=pltpu.PrefetchScalarGridSpec(
            num_scalar_prefetch=1,
            grid=(n_groups, n_heads),
            in_specs=[
                pl.BlockSpec((n_half, block, three_width), lambda t, j, me: (local_at, 0, t)),
                pl.BlockSpec((n_half, block, three_width), lambda t, j, me: (0, 0, t)),
            ],
            out_specs=[pl.BlockSpec((n_half, block, width), lambda t, j, me: (0, 0, t))] * 2,
            scratch_shapes=[pltpu.VMEM((n_slots, block, three_width), BF16), pltpu.VMEM((n_slots, block, width), BF16)],
        ),
        compiler_params=params(dimension_semantics=("arbitrary", "arbitrary")),
        cost_estimate=cost(pairs * block * block * window * 4, n_groups * n_slots * block * width * 8, pairs * block * block),
    )(me, qkv_local, qkv_remote)


def tail_kernel(keep, n_w, out_tile, tile, x0, x1, c_near, c_far, *refs):
    wout_refs, refs = refs[:2 * n_w], refs[2 * n_w:]
    up_refs, down_refs, refs = refs[:n_w], refs[n_w:2 * n_w], refs[2 * n_w:]
    (bout_ref, gain_ref, shift_ref, bup_ref, bdown_ref, out0, out1,
     x_buf, ctx, normed, wout_buf, up_buf, down_buf, acc, x_sem, c_sem, wout_sem, up_sem, down_sem) = refs
    rows_all, d_model = x_buf.shape
    block = rows_all // 2
    width = wout_refs[0].shape[0]
    out_steps = d_model // out_tile
    per_w = up_refs[0].shape[1] // tile
    steps = n_w * per_w

    def fetch_out(n, go):
        slot = lax.rem(n, 2)
        cols = pl.ds(pl.multiple_of(n * out_tile, out_tile), out_tile)
        for j, w in enumerate(wout_refs):
            copy = pltpu.make_async_copy(w.at[:, cols], wout_buf.at[slot, pl.ds(j * width, width)], wout_sem.at[slot, j])
            copy.start() if go else copy.wait()

    def fetch_mlp(n, go):
        slot = lax.rem(n, 2)
        for t in range(n_w if go else 1):
            def transfer(at):
                part = pl.ds(pl.multiple_of(at * tile, tile), tile)
                up = pltpu.make_async_copy(up_refs[t].at[:, part], up_buf.at[slot], up_sem.at[slot])
                down = pltpu.make_async_copy(down_refs[t].at[part, :], down_buf.at[slot], down_sem.at[slot])
                return up, down

            if go:
                @pl.when((n >= t * per_w) & (n < (t + 1) * per_w))
                def _():
                    for copy in transfer(n - t * per_w):
                        copy.start()
            else:
                for copy in transfer(0):
                    copy.wait()

    copies = []
    for j, c in enumerate((c_near, c_far)):
        for p in range(2):
            copies.append(pltpu.make_async_copy(
                c.at[p], ctx.at[pl.ds(p * block, block), pl.ds(j * n_w * width, n_w * width)], c_sem.at[j, p]))
    for c in copies:
        c.start()
    fetch_out(0, True)
    for p, x in enumerate((x0, x1)):
        copies.append(pltpu.make_async_copy(x.at[0], x_buf.at[pl.ds(p * block, block)], x_sem.at[p]))
        copies[-1].start()
    fetch_mlp(0, True)
    for c in copies:
        c.wait()

    @pl.loop(0, out_steps)
    def _(n):
        @pl.when(n + 1 < out_steps)
        def _():
            fetch_out(n + 1, True)

        fetch_out(n, False)
        cols = pl.ds(pl.multiple_of(n * out_tile, out_tile), out_tile)
        part = jnp.dot(ctx[...], wout_buf[lax.rem(n, 2)], preferred_element_type=F32) + bout_ref[:, cols].astype(F32)
        x_buf[:, cols] = (x_buf[:, cols].astype(F32) + part).astype(BF16)

    @pl.loop(0, rows_all // CHUNK)
    def _(r):
        rows = pl.ds(pl.multiple_of(r * CHUNK, CHUNK), CHUNK)
        resid = x_buf[rows, :]
        normed[rows, :] = normalize(resid, gain_ref[...], shift_ref[...])
        if keep:
            acc[rows, :] = resid.astype(F32) + bdown_ref[...].astype(F32)
        else:
            acc[rows, :] = jnp.zeros_like(acc[rows, :])

    @pl.loop(0, steps)
    def _(n):
        @pl.when(n + 1 < steps)
        def _():
            fetch_mlp(n + 1, True)

        fetch_mlp(n, False)
        slot = lax.rem(n, 2)
        up = jnp.dot(normed[...], up_buf[slot], preferred_element_type=F32) + bup_ref[n].astype(F32)
        act = jax.nn.gelu(up, approximate=True).astype(BF16)
        acc[...] += jnp.dot(act, down_buf[slot], preferred_element_type=F32)

    out0[...] = acc[0:block].astype(out0.dtype)
    out1[...] = acc[block:].astype(out1.dtype)


def tail(xs, c_near, c_far, w_outs, ups, downs, vectors, b_up, b_down, keep):
    _, block, d_model = xs[0].shape
    width = w_outs[0].shape[0]
    n_w = len(ups)
    n_cols = ups[0].shape[1]
    out_tile = tile = 512
    rows = 2 * block
    out = jax.ShapeDtypeStruct((block, d_model), F32 if keep else BF16)
    total = n_w * n_cols
    return pl.pallas_call(
        functools.partial(tail_kernel, keep, n_w, out_tile, tile),
        out_shape=[out, out],
        in_specs=[ANY] * (4 + 4 * n_w) + [WHOLE] * 5,
        out_specs=[WHOLE, WHOLE],
        scratch_shapes=[
            pltpu.VMEM((rows, d_model), BF16),
            pltpu.VMEM((rows, 2 * n_w * width), BF16),
            pltpu.VMEM((rows, d_model), BF16),
            pltpu.VMEM((2, 2 * n_w * width, out_tile), BF16),
            pltpu.VMEM((2, d_model, tile), BF16),
            pltpu.VMEM((2, tile, d_model), BF16),
            pltpu.VMEM((rows, d_model), F32),
            pltpu.SemaphoreType.DMA((2,)),
            pltpu.SemaphoreType.DMA((2, 2)),
            pltpu.SemaphoreType.DMA((2, 2 * n_w)),
            pltpu.SemaphoreType.DMA((2,)),
            pltpu.SemaphoreType.DMA((2,)),
        ],
        compiler_params=params(),
        cost_estimate=cost(
            2 * rows * d_model * (2 * n_w * width + 2 * total),
            2 * (rows * 4 * d_model + 2 * n_w * width * d_model + 2 * total * d_model),
            rows * total),
    )(*xs, c_near, c_far, *w_outs, *ups, *downs, *vectors, b_up.reshape(total // tile, 1, tile), b_down)


def finish_kernel(core_ref, base_ref, arrived_ref, *refs):
    out_ref = refs[-1]
    out_ref[...] = (base_ref[...] + arrived_ref[...].astype(F32)).astype(BF16).reshape(out_ref.shape)


def place_kernel(core_ref, block_ref, out_in_ref, out_ref):
    out_ref[0] = block_ref[...]


def finish(core, base, arrived, s, n_batch, out):
    block, d_model = base.shape
    n_mine = n_batch // 2
    tile = 128
    spec = pl.BlockSpec((tile, d_model), lambda i, c: (i, 0))
    extra = [] if out is None else [out]
    return pl.pallas_call(
        finish_kernel,
        out_shape=jax.ShapeDtypeStruct((n_batch, block, d_model), BF16),
        grid_spec=pltpu.PrefetchScalarGridSpec(
            num_scalar_prefetch=1,
            grid=(block // tile,),
            in_specs=[spec, spec] + [ANY] * len(extra),
            out_specs=pl.BlockSpec((1, tile, d_model), lambda i, c: (c[0] * n_mine + s, i, 0)),
        ),
        input_output_aliases={3: 0} if extra else {},
        compiler_params=params(),
        cost_estimate=cost(block * d_model * 2, 8 * block * d_model),
    )(core, base, arrived, *extra)


def finish_other(core, base, arrived):
    block, d_model = base.shape
    tile = 128
    spec = pl.BlockSpec((tile, d_model), lambda i, c: (i, 0))
    return pl.pallas_call(
        finish_kernel,
        out_shape=jax.ShapeDtypeStruct((block, d_model), BF16),
        grid_spec=pltpu.PrefetchScalarGridSpec(num_scalar_prefetch=1, grid=(block // tile,), in_specs=[spec, spec], out_specs=spec),
        compiler_params=params(),
        cost_estimate=cost(block * d_model * 2, 8 * block * d_model),
    )(core, base, arrived)


def place(core, piece, s, out):
    n_batch, block, d_model = out.shape
    n_mine = n_batch // 2
    tile = 128
    return pl.pallas_call(
        place_kernel,
        out_shape=jax.ShapeDtypeStruct(out.shape, BF16),
        grid_spec=pltpu.PrefetchScalarGridSpec(
            num_scalar_prefetch=1,
            grid=(block // tile,),
            in_specs=[pl.BlockSpec((tile, d_model), lambda i, c: (i, 0)), ANY],
            out_specs=pl.BlockSpec((1, tile, d_model), lambda i, c: ((1 - c[0]) * n_mine + s, i, 0)),
        ),
        input_output_aliases={2: 0},
        compiler_params=params(),
        cost_estimate=cost(block * d_model, 4 * block * d_model),
    )(core, piece, out)


def solution(mesh):
    group_size = mesh.shape["tp"]
    n_groups = mesh.shape["dp"]

    def swap(array, mask):
        return lax.ppermute(array, "tp", [(i, i ^ mask) for i in range(group_size)])

    def device_body(hidden, ln1_gain, ln1_bias, w_qkv, b_qkv, w_out, b_out, ln2_gain, ln2_bias, w_up, b_up, w_down, b_down):
        n_batch, _, d_model = hidden.shape
        _, _, n_heads, head_dim = w_qkv.shape
        width = n_heads * head_dim
        me = lax.axis_index("tp")
        core = me % 2
        group = lax.axis_index("dp")
        n_mine = n_batch // 2
        row = lambda v: v.reshape(1, -1)
        me_array = jnp.reshape(me, (1,)).astype(jnp.int32)
        core_array = jnp.reshape(core, (1,)).astype(jnp.int32)

        slots = [[None] * group_size for _ in range(n_mine)]
        others = []
        source = hidden
        for s in range(n_mine):
            slots[s][0] = lax.dynamic_slice_in_dim(source, core * n_mine + s, 1, 0)
            slots[s][2] = swap(slots[s][0], 2)
            source, _ = lax.optimization_barrier((source, slots[s][0]))
            others.append(lax.dynamic_slice_in_dim(source, (1 - core) * n_mine + s, 1, 0))
            slots[s][3] = swap(others[s], 3)
            slots[s][1] = swap(others[s], 1)
            source, _ = lax.optimization_barrier((source, others[s]))

        biases = jnp.concatenate([b_qkv.reshape(-1), b_up])
        biases_of = [biases, swap(biases, 1)]
        b_qkv_all = row(jnp.concatenate([b[:3 * width] for b in biases_of]))
        b_up_all = jnp.concatenate([b[3 * width:] for b in biases_of])
        w_qkv_t = jnp.transpose(w_qkv, (1, 2, 3, 0)).reshape(3 * width, d_model)
        w_qkv_of = [w_qkv_t, swap(w_qkv_t, 1)]
        w_out_flat = w_out.reshape(width, d_model)
        half_rows = width // n_groups
        near = swap(lax.dynamic_slice_in_dim(w_out_flat, group * half_rows, half_rows, 0), 2)
        far = lax.ppermute(near, "dp", [(i, (i + 1) % n_groups) for i in range(n_groups)])
        w_out2 = jnp.where(group == 0, jnp.concatenate([near, far]), jnp.concatenate([far, near]))
        w_out_of = [w_out_flat, swap(w_out_flat, 1), w_out2, swap(w_out2, 1)]
        w_up_of = [w_up, swap(w_up, 1)]
        w_down_of = [w_down, swap(w_down, 1)]

        gain1, shift1 = row(ln1_gain), row(ln1_bias)
        local = qkv_projection([x for s in range(n_mine) for x in slots[s][:2]], gain1, shift1, b_qkv_all, w_qkv_of)
        near_ctx, far_ctx, arrived_near, arrived_far = [], [], [], []
        for s in range(n_mine):
            remote = qkv_projection(slots[s][2:], gain1, shift1, b_qkv_all, w_qkv_of)
            a, b = attention(me_array, local, s, remote, 2, n_heads, head_dim)
            near_ctx.append(a)
            far_ctx.append(b)
            arrived_near.append(swap(a, 2))
            arrived_far.append(swap(b, 2))

        vectors = (row(b_out), row(ln2_gain), row(ln2_bias))
        from_other = []
        for s in range(n_mine):
            part2, part3 = tail(slots[s][2:], far_ctx[s], arrived_near[s], w_out_of, w_up_of, w_down_of, vectors, b_up_all, row(b_down), False)
            from_other.append((swap(part3, 2), swap(part2, 2)))
        bases = []
        for s in range(n_mine):
            bases.append(tail(slots[s][:2], near_ctx[s], arrived_far[s], w_out_of, w_up_of, w_down_of, vectors, b_up_all, row(b_down), True))
        out, pieces = None, []
        for s in range(n_mine):
            piece = finish_other(core_array, bases[s][1], from_other[s][0])
            pieces.append(swap(piece, 1))
            if s == n_mine - 1:
                for k in range(n_mine):
                    out = place(core_array, pieces[k], k, out)
            out = finish(core_array, bases[s][0], from_other[s][1], s, n_batch, out)
        return out

    in_layout = (P("dp", "tp", None), P(), P(), P(None, None, "tp", None), P(None, "tp", None), P("tp", None, None), P(), P(), P(), P(None, "tp"), P("tp"), P("tp", None), P())
    return jax.shard_map(device_body, mesh=mesh, in_specs=in_layout, out_specs=P("dp", "tp", None), check_vma=False)
```

time: 1170 us -> 538 us (0.46)
  waiting for transfers between devices: 715 us -> 139 us
  Pallas kernels: 0 us -> 352 us
  matrix products: 306 us -> 0 us
  other arithmetic: 76.2 us -> 3.58 us
  between operations: 13.8 us -> 0.29 us
  local copies, waits for them, and re-layouts: 35 us -> 22.5 us
    all_to_all x2 -> x0, waiting for transfers between devices: 456 us -> none  [scatter_sum(): received = lax.all_to_all(split_view, 'tp', 1, 1, tiled=True)]
    pallas_call x0 -> x15, Pallas kernels: none -> 352 us  [the longest x4 196 us: tail(): pl.pallas_call(functools.partial(tail_kernel, keep, n_w, out_tile, tile),...]
    all_gather x2 -> x0, waiting for transfers between devices: 259 us -> none  [the longest x1 130 us: device_body(): normed_all = lax.all_gather(normed, 'tp', axis=1, tiled=True)]
    dot_general x4 -> x0, matrix products: 246 us -> none  [the longest x1 69.9 us: device_body(): jnp.einsum('bsd,df->bsf', mid_all, w_up, preferred_element_type=jnp.float32)]
    ppermute x0 -> x24, waiting for transfers between devices: none -> 139 us  [the longest x23 114 us: swap(): return lax.ppermute(array, 'tp', [(i, i ^ mask) for i in range(group_size)])]
    sub x1 -> x0, matrix products: 60.3 us -> none  [causal_attention(): exp_vals = jnp.exp(logits - row_max)]
    reduce_sum x6 -> x0, other arithmetic: 53.4 us -> none  [the longest x2 32 us: scatter_sum(): return jnp.sum(received.astype(jnp.float32), axis=1)]
    reshape x2 -> x8, local copies, waits for them, and re-layouts: 35 us -> 4.35 us  [the longest x7 4.27 us: device_body(): row = lambda v: v.reshape(1, -1)]
  transfers between devices with their start and end apart: 4 -> 24, of which waited for: 4 -> 6; matrix products, arithmetic and copies ran while one was open for 0% -> 4% of each run, Pallas kernels for 0% -> 65%
where the time goes in v1:
time: 538 us; the launch traced here: 537 us
  Pallas kernels  352 us (65%)
  waiting for transfers between devices  139 us (26%)
  local copies, waits for them, and re-layouts  22.5 us (4%)
  starting transfers between devices  19.4 us (4%)
    pallas_call x4, Pallas kernels, tail(): pl.pallas_call(functools.partial(tail_kernel, keep, n_w, out_tile, tile),...  196 us
    ppermute x23, waiting for transfers between devices, swap(): return lax.ppermute(array, 'tp', [(i, i ^ mask) for i in range(group_size)])  114 us
    pallas_call x2, Pallas kernels, attention(): pl.pallas_call(functools.partial(attention_kernel, n_heads, head_dim, win...  72.7 us
    pallas_call x3, Pallas kernels, qkv_projection(): pl.pallas_call(functools.partial(qkv_kernel, n_x, n_w, tile), out_shape=j...  66.8 us
    ppermute x1, waiting for transfers between devices, device_body(): lax.ppermute(near, 'dp', [(i, (i + 1) % n_groups) for i in range(n_groups)])  25.2 us
    ppermute x23, starting transfers between devices, swap(): return lax.ppermute(array, 'tp', [(i, i ^ mask) for i in range(group_size)])  17.7 us
  transfers between devices with their start and end apart: 24, of which 6 were waited for; matrix products, arithmetic and copies ran while one was open for 4% of the time, Pallas kernels for 65%

profile of v1, /device:TPU:0, one launch (start us, length us, event | category | flops | bytes accessed | tf_op | source)
XLA Modules:
  0.0 537.2 jit_solution(5875494663461322130)
XLA Ops:
  0.0 0.8 collective-permute-start.3
  0.8 0.0 collective-permute-start.11
  0.8 0.5 collective-permute-start.12
  1.4 1.6 constant_dynamic-slice_fusion
  2.9 2.5 collective-permute-start.8
  5.4 36.5 %collective-permute-done.8 = bf16[320,2560]{1,0:T(8,128)(2,1)S(1)} collective-permute-done((bf16[320,2560]{1,0:T(8,128)(2,1)S(1)}, bf16[320,2560]{1,0:T(8,128)(2,1)S(1)}, u32[]{:S(2)}, u32[]{:S(2)}) %collective-permute-start.8) | collective-permute-done | bytes 1638432 | tf_op jit(solution)/shard_map/ppermute | solution.py:380
  41.9 1.8 collective-permute-start.9
  43.7 0.1 reshape.49
  43.8 0.0 collective-permute-start.2
  43.8 2.4 constant_dynamic-slice_fusion.4.refs_0_.x0
  46.3 2.5 constant_dynamic-slice_fusion.3
  48.8 2.5 constant_dynamic-slice_fusion.2.refs_2_.x0
  51.3 0.0 copy-start.11
  51.3 0.0 copy-start.12
  51.3 2.5 constant_dynamic-slice_fusion.1
  53.9 0.5 collective-permute-start
  54.3 25.2 %collective-permute-done.9 = bf16[320,2560]{1,0:T(8,128)(2,1)S(1)} collective-permute-done((bf16[320,2560]{1,0:T(8,128)(2,1)S(1)}, bf16[320,2560]{1,0:T(8,128)(2,1)S(1)}, u32[]{:S(2)}, u32[]{:S(2)}) %collective-permute-start.9) | collective-permute-done | bytes 1638432 | tf_op jit(solution)/shard_map/ppermute | solution.py:415
  79.5 0.7 reshape.53.refs_8_
  80.2 0.6 reshape.54.refs_9_
  80.8 0.6 reshape.55.refs_10_
  81.4 0.6 reshape.56.refs_12_
  82.0 0.6 reshape.47.refs_4_.refs_2_
  82.6 0.6 reshape.48.refs_5_.refs_3_
  83.3 0.6 reshape.50.refs_6_.refs_4_
  83.9 3.6 maximum_select_fusion.refs_2_
  87.5 1.5 collective-permute-start.5
  89.1 0.2 collective-permute-start.18
  89.3 1.5 collective-permute-start.17
  90.8 31.4 %shard_map.127.local_ref = bf16[4,256,3840]{2,1,0:T(8,128)(2,1)} custom-call(bf16[1,256,2560]{2,1,0:T(8,128)(2,1)} %constant_dynamic-slice_fusion.4.refs_0_.x0, bf16[1,256,2560]{2,1,0:T(8,128)(2,1)} %collective-permute-done.1.refs_1_.x1, bf16[1,256,2560]{2,1,0:T(8,128)(2,1)} %constant_dynamic-slice_fusion.2.refs_2_.x0, ...), custom_call_target="tpu_custom_call" | custom-call | flops 20132659200 | bytes 32768000 | tf_op jit(solution)/shard_map/pallas_call | solution.py:92
  122.2 0.6 collective-permute-start.4
  122.8 23.8 %collective-permute-done.18.refs_1_.x1 = bf16[1,256,2560]{2,1,0:T(8,128)(2,1)} collective-permute-done((bf16[1,256,2560]{2,1,0:T(8,128)(2,1)}, bf16[1,256,2560]{2,1,0:T(8,128)(2,1)}, u32[]{:S(2)}, u32[]{:S(2)}) %collective-permute-start.18) | collective-permute-done | bytes 1310752 | tf_op jit(solution)/shard_map/ppermute | solution.py:380
  146.6 0.8 collective-permute-start.7
  147.5 28.3 %collective-permute-done.17.refs_0_.x0 = bf16[1,256,2560]{2,1,0:T(8,128)(2,1)} collective-permute-done((bf16[1,256,2560]{2,1,0:T(8,128)(2,1)}, bf16[1,256,2560]{2,1,0:T(8,128)(2,1)}, u32[]{:S(2)}, u32[]{:S(2)}) %collective-permute-start.17) | collective-permute-done | bytes 1310752 | tf_op jit(solution)/shard_map/ppermute | solution.py:380
  175.8 17.7 %shard_map.133.remote_ref = bf16[2,256,3840]{2,1,0:T(8,128)(2,1)} custom-call(bf16[1,256,2560]{2,1,0:T(8,128)(2,1)} %collective-permute-done.17.refs_0_.x0, bf16[1,256,2560]{2,1,0:T(8,128)(2,1)} %collective-permute-done.18.refs_1_.x1, f32[1,2560]{1,0:T(1,128)} %reshape.47.refs_4_.refs_2_, f32[1,2560]{1,0:T(1,128)} %reshape.48.refs_5_.refs_3_, ...), custom_call_target="tpu_custom_call" | custom-call | flops 10066329600 | bytes 26214400 | tf_op jit(solution)/shard_map/pallas_call | solution.py:92
  193.4 36.3 %shard_map.134 = (bf16[2,256,1280]{2,1,0:T(8,128)(2,1)}, bf16[2,256,1280]{2,1,0:T(8,128)(2,1)}) custom-call(s32[1]{0:T(128)} %bitcast.1.me_ref, bf16[4,256,3840]{2,1,0:T(8,128)(2,1)} %shard_map.127.local_ref, bf16[2,256,3840]{2,1,0:T(8,128)(2,1)} %shard_map.133.remote_ref), custom_call_target="tpu_custom_call" | custom-call | flops 10737418240 | bytes 10485760 | tf_op jit(solution)/shard_map/pallas_call | solution.py:170
  229.7 1.5 collective-permute-start.20
  231.2 17.7 %shard_map.128.remote_ref = bf16[2,256,3840]{2,1,0:T(8,128)(2,1)} custom-call(bf16[1,256,2560]{2,1,0:T(8,128)(2,1)} %collective-permute-done.4.refs_0_.x0, bf16[1,256,2560]{2,1,0:T(8,128)(2,1)} %collective-permute-done.5.refs_1_.x1, f32[1,2560]{1,0:T(1,128)} %reshape.47.refs_4_.refs_2_, f32[1,2560]{1,0:T(1,128)} %reshape.48.refs_5_.refs_3_, ...), custom_call_target="tpu_custom_call" | custom-call | flops 10066329600 | bytes 26214400 | tf_op jit(solution)/shard_map/pallas_call | solution.py:92
  248.9 36.4 %shard_map.129 = (bf16[2,256,1280]{2,1,0:T(8,128)(2,1)}, bf16[2,256,1280]{2,1,0:T(8,128)(2,1)}) custom-call(s32[1]{0:T(128)} %bitcast.1.me_ref, bf16[4,256,3840]{2,1,0:T(8,128)(2,1)} %shard_map.127.local_ref, bf16[2,256,3840]{2,1,0:T(8,128)(2,1)} %shard_map.128.remote_ref), custom_call_target="tpu_custom_call" | custom-call | flops 10737418240 | bytes 10485760 | tf_op jit(solution)/shard_map/pallas_call | solution.py:170
  285.2 0.6 collective-permute-start.19
  285.8 1.5 collective-permute-start.13
  287.3 0.6 collective-permute-start.6
  287.8 48.7 %shard_map.136 = (bf16[256,2560]{1,0:T(8,128)(2,1)}, bf16[256,2560]{1,0:T(8,128)(2,1)}) custom-call(bf16[1,256,2560]{2,1,0:T(8,128)(2,1)} %collective-permute-done.17.refs_0_.x0, bf16[1,256,2560]{2,1,0:T(8,128)(2,1)} %collective-permute-done.18.refs_1_.x1, bf16[2,256,1280]{2,1,0:T(8,128)(2,1)} %get-tuple-element.30.c_near, ...), custom_call_target="tpu_custom_call" | custom-call | flops 33554432000 | bytes 76021760 | tf_op jit(solution)/shard_map/pallas_call | solution.py:286
  336.6 1.5 collective-permute-start.21
  338.0 0.6 collective-permute-start.23
  338.6 6.6 %collective-permute-done.13.c_far = bf16[2,256,1280]{2,1,0:T(8,128)(2,1)S(1)} collective-permute-done((bf16[2,256,1280]{2,1,0:T(8,128)(2,1)}, bf16[2,256,1280]{2,1,0:T(8,128)(2,1)S(1)}, u32[]{:S(2)}, u32[]{:S(2)}) %collective-permute-start.13) | collective-permute-done | bytes 1310752 | tf_op jit(solution)/shard_map/ppermute | solution.py:380
  345.2 1.1 copy-done.17
  346.2 48.6 %shard_map.131 = (bf16[256,2560]{1,0:T(8,128)(2,1)}, bf16[256,2560]{1,0:T(8,128)(2,1)}) custom-call(bf16[1,256,2560]{2,1,0:T(8,128)(2,1)} %collective-permute-done.4.refs_0_.x0, bf16[1,256,2560]{2,1,0:T(8,128)(2,1)} %collective-permute-done.5.refs_1_.x1, bf16[2,256,1280]{2,1,0:T(8,128)(2,1)} %get-tuple-element.24.c_near, bf16[2,256,1280]{2,1,0:T(8,128)(2,1)} %copy-done.17, ...), custom_call_target="tpu_custom_call" | custom-call | flops 33554432000 | bytes 76021760 | tf_op jit(solution)/shard_map/pallas_call | solution.py:286
  394.8 0.6 collective-permute-start.15
  395.4 49.4 %shard_map.135 = (f32[256,2560]{1,0:T(8,128)}, f32[256,2560]{1,0:T(8,128)}) custom-call(bf16[1,256,2560]{2,1,0:T(8,128)(2,1)} %constant_dynamic-slice_fusion.4.refs_0_.x0, bf16[1,256,2560]{2,1,0:T(8,128)(2,1)} %collective-permute-done.1.refs_1_.x1, bf16[2,256,1280]{2,1,0:T(8,128)(2,1)} %get-tuple-element.29.c_near, ...), custom_call_target="tpu_custom_call" | custom-call | flops 33554432000 | bytes 76021760 | tf_op jit(solution)/shard_map/pallas_call | solution.py:286
  444.8 49.6 %shard_map.130 = (f32[256,2560]{1,0:T(8,128)}, f32[256,2560]{1,0:T(8,128)}) custom-call(bf16[1,256,2560]{2,1,0:T(8,128)(2,1)} %constant_dynamic-slice_fusion.2.refs_2_.x0, bf16[1,256,2560]{2,1,0:T(8,128)(2,1)} %collective-permute-done.refs_3_.x1, bf16[2,256,1280]{2,1,0:T(8,128)(2,1)} %get-tuple-element.23.c_near, ...), custom_call_target="tpu_custom_call" | custom-call | flops 33554432000 | bytes 76021760 | tf_op jit(solution)/shard_map/pallas_call | solution.py:286
  494.4 1.1 copy-done.6
  495.5 3.0 shard_map.137
  498.6 1.1 copy-done.7
  499.6 3.1 shard_map.132
  502.7 0.5 collective-permute-start.16
  503.2 1.5 collective-permute-start.14
  504.7 1.1 copy-done.3
  505.7 3.0 shard_map.138.out_in_ref
  508.8 1.1 copy-done.4
  509.9 2.2 shard_map.139.out_in_ref
  512.0 1.1 copy-done.5
  513.1 2.2 shard_map.140.refs_0_
  515.3 18.9 %collective-permute-done.14.arrived_ref = bf16[256,2560]{1,0:T(8,128)(2,1)} collective-permute-done((bf16[256,2560]{1,0:T(8,128)(2,1)}, bf16[256,2560]{1,0:T(8,128)(2,1)}, u32[]{:S(2)}, u32[]{:S(2)}) %collective-permute-start.14) | collective-permute-done | bytes 1310752 | tf_op jit(solution)/shard_map/ppermute | solution.py:380
  534.2 3.0 shard_map.141
  (57 shorter events, 0.2 us)
Async XLA Ops:
  0.0 89.3 %collective-permute-start.3 = (bf16[1920,2560]{1,0:T(8,128)(2,1)}, bf16[1920,2560]{1,0:T(8,128)(2,1)}, u32[]{:S(2)}, u32[]{:S(2)}) collective-permute-start(bf16[1920,2560]{1,0:T(8,128)(2,1)} %bitcast.12), channel_id=1, source_target_pairs={{0,1},{1,0},{2,3},{3,2},{4,5},{5,4},{6,7},{7,6}} | collective-permute-start | bytes 29491208 | tf_op jit(solution)/shard_map/ppermute | solution.py:380
  0.8 287.0 %collective-permute-start.11 = (bf16[2560,2560]{1,0:T(8,128)(2,1)}, bf16[2560,2560]{1,0:T(8,128)(2,1)}, u32[]{:S(2)}, u32[]{:S(2)}) collective-permute-start(bf16[2560,2560]{1,0:T(8,128)(2,1)} %refs_4_.7), channel_id=1, source_target_pairs={{0,1},{1,0},{2,3},{3,2},{4,5},{5,4},{6,7},{7,6}} | collective-permute-start | bytes 39321608 | tf_op jit(solution)/shard_map/ppermute | solution.py:380
  0.8 287.0 %collective-permute-start.12 = (bf16[2560,2560]{1,0:T(8,128)(2,1)}, bf16[2560,2560]{1,0:T(8,128)(2,1)}, u32[]{:S(2)}, u32[]{:S(2)}) collective-permute-start(bf16[2560,2560]{1,0:T(8,128)(2,1)} %refs_6_.7), channel_id=1, source_target_pairs={{0,1},{1,0},{2,3},{3,2},{4,5},{5,4},{6,7},{7,6}} | collective-permute-start | bytes 39321608 | tf_op jit(solution)/shard_map/ppermute | solution.py:380
  1.3 42.3 %copy-start.13 = (bf16[3,8,80]{2,1,0:T(8,128)(2,1)S(1)}, bf16[3,8,80]{2,1,0:T(8,128)(2,1)}, u32[]{:S(2)}) copy-start(bf16[3,8,80]{2,1,0:T(8,128)(2,1)} %param.17) | copy-start | bytes 11524
  1.3 42.4 %copy-start.8 = (bf16[2560]{0:T(1024)(128)(2,1)S(1)}, bf16[2560]{0:T(1024)(128)(2,1)}, u32[]{:S(2)}) copy-start(bf16[2560]{0:T(1024)(128)(2,1)} %param.23) | copy-start | bytes 15364
  2.9 39.0 %collective-permute-start.8 = (bf16[320,2560]{1,0:T(8,128)(2,1)S(1)}, bf16[320,2560]{1,0:T(8,128)(2,1)S(1)}, u32[]{:S(2)}, u32[]{:S(2)}) collective-permute-start(bf16[320,2560]{1,0:T(8,128)(2,1)S(1)} %constant_dynamic-slice_fusion), channel_id=1, source_target_pairs={{0,2},{1,3},{2,0},{3,1},{4,6},{5,7},{6,4},{7,5}} | collective-permute-start | bytes 4915208 | tf_op jit(solution)/shard_map/ppermute | solution.py:380
  41.9 6.9 %copy-start.1 = (bf16[320,2560]{1,0:T(8,128)(2,1)}, bf16[320,2560]{1,0:T(8,128)(2,1)S(1)}, u32[]{:S(2)}) copy-start(bf16[320,2560]{1,0:T(8,128)(2,1)S(1)} %collective-permute-done.8) | copy-start | bytes 4915204
  41.9 37.6 %collective-permute-start.9 = (bf16[320,2560]{1,0:T(8,128)(2,1)S(1)}, bf16[320,2560]{1,0:T(8,128)(2,1)S(1)}, u32[]{:S(2)}, u32[]{:S(2)}) collective-permute-start(bf16[320,2560]{1,0:T(8,128)(2,1)S(1)} %collective-permute-done.8), channel_id=1, source_target_pairs={{0,4},{4,0},{1,5},{5,1},{2,6},{6,2},{3,7},{7,3}} | collective-permute-start | bytes 4915208 | tf_op jit(solution)/shard_map/ppermute | solution.py:415
  43.8 10.1 %collective-permute-start.2 = (bf16[4480]{0:T(1024)(128)(2,1)S(1)}, bf16[4480]{0:T(1024)(128)(2,1)S(1)}, u32[]{:S(2)}, u32[]{:S(2)}) collective-permute-start(bf16[4480]{0:T(1024)(128)(2,1)S(1)} %pad_maximum_fusion), channel_id=1, source_target_pairs={{0,1},{1,0},{2,3},{3,2},{4,5},{5,4},{6,7},{7,6}} | collective-permute-start | bytes 26888 | tf_op jit(solution)/shard_map/ppermute | solution.py:380
  51.3 28.3 %copy-start.14 = (bf16[2560]{0:T(1024)(128)(2,1)S(1)}, bf16[2560]{0:T(1024)(128)(2,1)}, u32[]{:S(2)}) copy-start(bf16[2560]{0:T(1024)(128)(2,1)} %param.19) | copy-start | bytes 15364
  51.3 28.9 %copy-start.9 = (f32[2560]{0:T(1024)S(1)}, f32[2560]{0:T(1024)}, u32[]{:S(2)}) copy-start(f32[2560]{0:T(1024)} %param.20) | copy-start | bytes 30724
  51.3 29.5 %copy-start.10 = (f32[2560]{0:T(1024)S(1)}, f32[2560]{0:T(1024)}, u32[]{:S(2)}) copy-start(f32[2560]{0:T(1024)} %param.21) | copy-start | bytes 30724
  51.3 30.1 %copy-start.15 = (bf16[2560]{0:T(1024)(128)(2,1)S(1)}, bf16[2560]{0:T(1024)(128)(2,1)}, u32[]{:S(2)}) copy-start(bf16[2560]{0:T(1024)(128)(2,1)} %param.25) | copy-start | bytes 15364
  51.3 30.7 %copy-start.11 = (f32[2560]{0:T(1024)S(1)}, f32[2560]{0:T(1024)}, u32[]{:S(2)}) copy-start(f32[2560]{0:T(1024)} %param.14) | copy-start | bytes 30724
  51.3 31.3 %copy-start.12 = (f32[2560]{0:T(1024)S(1)}, f32[2560]{0:T(1024)}, u32[]{:S(2)}) copy-start(f32[2560]{0:T(1024)} %param.15) | copy-start | bytes 30724
  53.9 33.7 %collective-permute-start = (bf16[1,256,2560]{2,1,0:T(8,128)(2,1)}, bf16[1,256,2560]{2,1,0:T(8,128)(2,1)}, u32[]{:S(2)}, u32[]{:S(2)}) collective-permute-start(bf16[1,256,2560]{2,1,0:T(8,128)(2,1)} %constant_dynamic-slice_fusion.1), channel_id=1, source_target_pairs={{0,1},{1,0},{2,3},{3,2},{4,5},{5,4},{6,7},{7,6}} | collective-permute-start | bytes 3932168 | tf_op jit(solution)/shard_map/ppermute | solution.py:380
  79.5 4.4 copy-start.2
  79.5 9.5 %collective-permute-start.1 = (bf16[1,256,2560]{2,1,0:T(8,128)(2,1)}, bf16[1,256,2560]{2,1,0:T(8,128)(2,1)}, u32[]{:S(2)}, u32[]{:S(2)}) collective-permute-start(bf16[1,256,2560]{2,1,0:T(8,128)(2,1)} %constant_dynamic-slice_fusion.3), channel_id=1, source_target_pairs={{0,1},{1,0},{2,3},{3,2},{4,5},{5,4},{6,7},{7,6}} | collective-permute-start | bytes 3932168 | tf_op jit(solution)/shard_map/ppermute | solution.py:380
  83.9 3.6 copy-start.16
  87.5 88.2 %copy-start = (bf16[640,2560]{1,0:T(8,128)(2,1)}, bf16[640,2560]{1,0:T(8,128)(2,1)S(1)}, u32[]{:S(2)}) copy-start(bf16[640,2560]{1,0:T(8,128)(2,1)S(1)} %maximum_select_fusion.refs_2_) | copy-start | bytes 9830404
  87.5 34.7 %collective-permute-start.5 = (bf16[1,256,2560]{2,1,0:T(8,128)(2,1)}, bf16[1,256,2560]{2,1,0:T(8,128)(2,1)}, u32[]{:S(2)}, u32[]{:S(2)}) collective-permute-start(bf16[1,256,2560]{2,1,0:T(8,128)(2,1)} %constant_dynamic-slice_fusion.1), channel_id=1, source_target_pairs={{0,3},{1,2},{2,1},{3,0},{4,7},{5,6},{6,5},{7,4}} | collective-permute-start | bytes 3932168 | tf_op jit(solution)/shard_map/ppermute | solution.py:380
  89.1 57.6 %collective-permute-start.18 = (bf16[1,256,2560]{2,1,0:T(8,128)(2,1)}, bf16[1,256,2560]{2,1,0:T(8,128)(2,1)}, u32[]{:S(2)}, u32[]{:S(2)}) collective-permute-start(bf16[1,256,2560]{2,1,0:T(8,128)(2,1)} %constant_dynamic-slice_fusion.3), channel_id=1, source_target_pairs={{0,3},{1,2},{2,1},{3,0},{4,7},{5,6},{6,5},{7,4}} | collective-permute-start | bytes 3932168 | tf_op jit(solution)/shard_map/ppermute | solution.py:380
  89.3 86.4 %collective-permute-start.17 = (bf16[1,256,2560]{2,1,0:T(8,128)(2,1)}, bf16[1,256,2560]{2,1,0:T(8,128)(2,1)}, u32[]{:S(2)}, u32[]{:S(2)}) collective-permute-start(bf16[1,256,2560]{2,1,0:T(8,128)(2,1)} %constant_dynamic-slice_fusion.4.refs_0_.x0), channel_id=1, source_target_pairs={{0,2},{1,3},{2,0},{3,1},{4,6},{5,7},{6,4},{7,5}} | collective-permute-start | bytes 3932168 | tf_op jit(solution)/shard_map/ppermute | solution.py:380
  122.2 107.5 %collective-permute-start.4 = (bf16[1,256,2560]{2,1,0:T(8,128)(2,1)}, bf16[1,256,2560]{2,1,0:T(8,128)(2,1)}, u32[]{:S(2)}, u32[]{:S(2)}) collective-permute-start(bf16[1,256,2560]{2,1,0:T(8,128)(2,1)} %constant_dynamic-slice_fusion.2.refs_2_.x0), channel_id=1, source_target_pairs={{0,2},{1,3},{2,0},{3,1},{4,6},{5,7},{6,4},{7,5}} | collective-permute-start | bytes 3932168 | tf_op jit(solution)/shard_map/ppermute | solution.py:380
  146.6 138.6 %collective-permute-start.7 = (bf16[640,2560]{1,0:T(8,128)(2,1)}, bf16[640,2560]{1,0:T(8,128)(2,1)}, u32[]{:S(2)}, u32[]{:S(2)}) collective-permute-start(bf16[640,2560]{1,0:T(8,128)(2,1)} %bitcast.7), channel_id=1, source_target_pairs={{0,1},{1,0},{2,3},{3,2},{4,5},{5,4},{6,7},{7,6}} | collective-permute-start | bytes 9830408 | tf_op jit(solution)/shard_map/ppermute | solution.py:380
  175.8 110.0 %collective-permute-start.10 = (bf16[640,2560]{1,0:T(8,128)(2,1)S(1)}, bf16[640,2560]{1,0:T(8,128)(2,1)}, u32[]{:S(2)}, u32[]{:S(2)}) collective-permute-start(bf16[640,2560]{1,0:T(8,128)(2,1)S(1)} %maximum_select_fusion.refs_2_), channel_id=1, source_target_pairs={{0,1},{1,0},{2,3},{3,2},{4,5},{5,4},{6,7},{7,6}} | collective-permute-start | bytes 9830408 | tf_op jit(solution)/shard_map/ppermute | solution.py:380
  229.7 57.5 %collective-permute-start.20 = (bf16[2,256,1280]{2,1,0:T(8,128)(2,1)}, bf16[2,256,1280]{2,1,0:T(8,128)(2,1)}, u32[]{:S(2)}, u32[]{:S(2)}) collective-permute-start(bf16[2,256,1280]{2,1,0:T(8,128)(2,1)} %get-tuple-element.29.c_near), channel_id=1, source_target_pairs={{0,2},{1,3},{2,0},{3,1},{4,6},{5,7},{6,4},{7,5}} | collective-permute-start | bytes 3932168 | tf_op jit(solution)/shard_map/ppermute | solution.py:380
  285.2 110.2 %collective-permute-start.19 = (bf16[2,256,1280]{2,1,0:T(8,128)(2,1)}, bf16[2,256,1280]{2,1,0:T(8,128)(2,1)}, u32[]{:S(2)}, u32[]{:S(2)}) collective-permute-start(bf16[2,256,1280]{2,1,0:T(8,128)(2,1)} %get-tuple-element.30.c_near), channel_id=1, source_target_pairs={{0,2},{1,3},{2,0},{3,1},{4,6},{5,7},{6,4},{7,5}} | collective-permute-start | bytes 3932168 | tf_op jit(solution)/shard_map/ppermute | solution.py:380
  285.8 59.4 %collective-permute-start.13 = (bf16[2,256,1280]{2,1,0:T(8,128)(2,1)}, bf16[2,256,1280]{2,1,0:T(8,128)(2,1)S(1)}, u32[]{:S(2)}, u32[]{:S(2)}) collective-permute-start(bf16[2,256,1280]{2,1,0:T(8,128)(2,1)} %get-tuple-element.23.c_near), channel_id=1, source_target_pairs={{0,2},{1,3},{2,0},{3,1},{4,6},{5,7},{6,4},{7,5}} | collective-permute-start | bytes 3932168 | tf_op jit(solution)/shard_map/ppermute | solution.py:380
  287.3 157.5 %collective-permute-start.6 = (bf16[2,256,1280]{2,1,0:T(8,128)(2,1)}, bf16[2,256,1280]{2,1,0:T(8,128)(2,1)}, u32[]{:S(2)}, u32[]{:S(2)}) collective-permute-start(bf16[2,256,1280]{2,1,0:T(8,128)(2,1)} %get-tuple-element.24.c_near), channel_id=1, source_target_pairs={{0,2},{1,3},{2,0},{3,1},{4,6},{5,7},{6,4},{7,5}} | collective-permute-start | bytes 3932168 | tf_op jit(solution)/shard_map/ppermute | solution.py:380
  336.6 157.8 %collective-permute-start.21 = (bf16[256,2560]{1,0:T(8,128)(2,1)}, bf16[256,2560]{1,0:T(8,128)(2,1)S(1)}, u32[]{:S(2)}, u32[]{:S(2)}) collective-permute-start(bf16[256,2560]{1,0:T(8,128)(2,1)} %get-tuple-element.32), channel_id=1, source_target_pairs={{0,2},{1,3},{2,0},{3,1},{4,6},{5,7},{6,4},{7,5}} | collective-permute-start | bytes 3932168 | tf_op jit(solution)/shard_map/ppermute | solution.py:380
  338.0 166.6 %collective-permute-start.23 = (bf16[256,2560]{1,0:T(8,128)(2,1)}, bf16[256,2560]{1,0:T(8,128)(2,1)S(1)}, u32[]{:S(2)}, u32[]{:S(2)}) collective-permute-start(bf16[256,2560]{1,0:T(8,128)(2,1)} %get-tuple-element.34), channel_id=1, source_target_pairs={{0,2},{1,3},{2,0},{3,1},{4,6},{5,7},{6,4},{7,5}} | collective-permute-start | bytes 3932168 | tf_op jit(solution)/shard_map/ppermute | solution.py:380
  345.2 1.1 copy-start.17
  394.8 103.7 %collective-permute-start.15 = (bf16[256,2560]{1,0:T(8,128)(2,1)}, bf16[256,2560]{1,0:T(8,128)(2,1)S(1)}, u32[]{:S(2)}, u32[]{:S(2)}) collective-permute-start(bf16[256,2560]{1,0:T(8,128)(2,1)} %get-tuple-element.28), channel_id=1, source_target_pairs={{0,2},{1,3},{2,0},{3,1},{4,6},{5,7},{6,4},{7,5}} | collective-permute-start | bytes 3932168 | tf_op jit(solution)/shard_map/ppermute | solution.py:380
  494.4 1.1 copy-start.6
  498.5 10.2 %collective-permute-start.22 = (bf16[256,2560]{1,0:T(8,128)(2,1)}, bf16[256,2560]{1,0:T(8,128)(2,1)S(1)}, u32[]{:S(2)}, u32[]{:S(2)}) collective-permute-start(bf16[256,2560]{1,0:T(8,128)(2,1)} %shard_map.137), channel_id=1, source_target_pairs={{0,1},{1,0},{2,3},{3,2},{4,5},{5,4},{6,7},{7,6}} | collective-permute-start | bytes 3932168 | tf_op jit(solution)/shard_map/ppermute | solution.py:380
  498.5 1.1 copy-start.7
  502.7 9.4 %collective-permute-start.16 = (bf16[256,2560]{1,0:T(8,128)(2,1)}, bf16[256,2560]{1,0:T(8,128)(2,1)S(1)}, u32[]{:S(2)}, u32[]{:S(2)}) collective-permute-start(bf16[256,2560]{1,0:T(8,128)(2,1)} %shard_map.132), channel_id=1, source_target_pairs={{0,1},{1,0},{2,3},{3,2},{4,5},{5,4},{6,7},{7,6}} | collective-permute-start | bytes 3932168 | tf_op jit(solution)/shard_map/ppermute | solution.py:380
  503.2 31.0 %collective-permute-start.14 = (bf16[256,2560]{1,0:T(8,128)(2,1)}, bf16[256,2560]{1,0:T(8,128)(2,1)}, u32[]{:S(2)}, u32[]{:S(2)}) collective-permute-start(bf16[256,2560]{1,0:T(8,128)(2,1)} %get-tuple-element.26), channel_id=1, source_target_pairs={{0,2},{1,3},{2,0},{3,1},{4,6},{5,7},{6,4},{7,5}} | collective-permute-start | bytes 3932168 | tf_op jit(solution)/shard_map/ppermute | solution.py:380
  504.7 1.1 copy-start.3
  508.8 1.1 copy-start.4
  512.0 1.1 copy-start.5
